TPU v7x, 32 devices: a whole 2x2x4 slice. The times are simulated.
32 devices in a mesh: fsdp: 8 (over z, x), grp: 4 (over y, core).
Axes of the slice: x: 2, y: 2, z: 4, core: 2. Of those that a mesh axis runs over, the one named last changes fastest.
Arguments:
- gradient: bfloat16 [24, 512, 512], P('fsdp', 'grp'), may hold values from -6 to 6
- left_factor: bfloat16 [96, 512, 512], P(('fsdp', 'grp'))
- right_factor: bfloat16 [96, 512, 512], P(('fsdp', 'grp'))
- block_owner: int32 [24], replicated, may hold values from 0 to 31, as said below
Outputs:
- preconditioned: bfloat16 [24, 512, 512], P('fsdp', 'grp')
Inputs may be any that keep to these rules, and one draw needn't show every extreme that they name: block_owner[b] is a device index, fsdp index times 4 plus grp index. The 3 blocks homed at one fsdp index go to devices of 3 different fsdp indices; the devices of each fsdp index own 3 blocks in all; no device owns more than 3 blocks, and at every fsdp index one device owns exactly 3.
All inputs are finite; a program needn't handle non-finite values.
Results may differ from a plain program's by a relative error of at most 0.0049.
Values may be sent and summed in bfloat16 or wider, within the bound.
A program may use at most 64 MiB of HBM per device.

v0:
```python
import jax
import jax.numpy as jnp
from jax import lax
from jax.sharding import PartitionSpec as P


def per_device(gradient, left_factor, right_factor, block_owner):
    local_blocks = gradient.shape[0]
    piece_rows = gradient.shape[1]
    block_width = gradient.shape[2]
    slot_count = left_factor.shape[0]
    columns = lax.axis_size("fsdp")
    groups = lax.axis_size("grp")
    column = lax.axis_index("fsdp")
    owners_all = block_owner.reshape(columns, local_blocks)
    dest_column = owners_all // groups
    dest_group = owners_all % groups
    mine_column = lax.dynamic_index_in_dim(dest_column, column, 0, keepdims=False)
    column_ids = jnp.arange(columns, dtype=jnp.int32)
    matching = mine_column[None, :] == column_ids[:, None]
    pick_send = matching.astype(jnp.bfloat16)
    outgoing = jnp.einsum(
        "cj,jrd->crd", pick_send, gradient, preferred_element_type=jnp.float32
    ).astype(jnp.bfloat16)
    arrived = lax.all_to_all(
        outgoing.reshape(columns * piece_rows, block_width),
        "fsdp",
        split_axis=0,
        concat_axis=0,
        tiled=True,
    )
    arrived = arrived.reshape(columns, piece_rows, block_width)
    toward = dest_column == column
    live_source = jnp.sum(toward.astype(jnp.int32), axis=1) > 0
    target = jnp.sum(jnp.where(toward, dest_group, 0), axis=1)
    same_owner = (target[None, :] == target[:, None]) & live_source[None, :] & live_source[:, None]
    before = column_ids[None, :] < column_ids[:, None]
    rank_slot = jnp.sum((same_owner & before).astype(jnp.int32), axis=1)
    group_ids = jnp.arange(groups, dtype=jnp.int32)
    slot_ids = jnp.arange(slot_count, dtype=jnp.int32)
    routing = (
        live_source[None, None, :]
        & (target[None, None, :] == group_ids[:, None, None])
        & (rank_slot[None, None, :] == slot_ids[None, :, None])
    )
    routing = routing.astype(jnp.bfloat16)
    packed = jnp.einsum(
        "oks,srd->kord", routing, arrived, preferred_element_type=jnp.float32
    ).astype(jnp.bfloat16)
    packed = packed.reshape(slot_count, groups * piece_rows, block_width)
    blocks = lax.all_to_all(packed, "grp", split_axis=1, concat_axis=1, tiled=True)
    left_product = jnp.einsum(
        "kab,kbc->kac", left_factor, blocks, preferred_element_type=jnp.float32
    ).astype(jnp.bfloat16)
    result = jnp.einsum(
        "kab,kbc->kac", left_product, right_factor, preferred_element_type=jnp.float32
    ).astype(jnp.bfloat16)
    returned = lax.all_to_all(result, "grp", split_axis=1, concat_axis=1, tiled=True)
    returned = returned.reshape(slot_count, groups, piece_rows, block_width)
    unpacked = jnp.einsum(
        "oks,kord->srd", routing, returned, preferred_element_type=jnp.float32
    ).astype(jnp.bfloat16)
    homeward = lax.all_to_all(
        unpacked.reshape(columns * piece_rows, block_width),
        "fsdp",
        split_axis=0,
        concat_axis=0,
        tiled=True,
    )
    homeward = homeward.reshape(columns, piece_rows, block_width)
    return jnp.einsum(
        "cj,crd->jrd", pick_send, homeward, preferred_element_type=jnp.float32
    ).astype(jnp.bfloat16)


def solution(mesh):
    return jax.shard_map(
        per_device,
        mesh=mesh,
        in_specs=(
            P("fsdp", "grp", None),
            P(("fsdp", "grp"), None, None),
            P(("fsdp", "grp"), None, None),
            P(),
        ),
        out_specs=P("fsdp", "grp", None),
        check_vma=False,
    )
```

profile of v0, /device:TPU:0, one launch (start us, length us, event | category | flops | bytes accessed | tf_op | source)
XLA Modules:
  0.0 135.2 jit_solution(5954696607277778726)
XLA Ops:
  0.0 0.0 copy-start
  0.0 0.8 reshape.94
  0.9 1.6 %convolution_convert_fusion.3 = bf16[8,128,512]{2,0,1:T(8,128)(2,1)S(1)} fusion(bf16[3,128,512]{2,1,0:T(8,128)(2,1)} %param.4, s32[3]{0:T(128)S(1)} %dynamic-slice_bitcast_fusion), kind=kOutput, calls=%fused_computation.7 | convolution fusion | flops 3670040 | bytes 1441804 | tf_op jit(solution)/shard_map/cj,jrd->crd/dot_general | solution.py:22
  2.5 1.3 copy.33
  3.8 7.3 %all-to-all-start = ((bf16[8,128,512]{2,1,0:T(8,128)(2,1)}), bf16[8,128,512]{2,1,0:T(8,128)(2,1)S(1)}, u32[]{:S(2)}, u32[]{:S(2)}) async-start(bf16[8,128,512]{2,1,0:T(8,128)(2,1)} %copy.33), calls=%async_computation | async-start | bytes 2097152 | tf_op jit(solution)/shard_map/all_to_all | solution.py:25
  11.1 0.1 convert_reduce_fusion.1
  11.2 0.2 convert_reduce_fusion
  11.4 25.4 %all-to-all-done = bf16[8,128,512]{2,1,0:T(8,128)(2,1)S(1)} async-done(((bf16[8,128,512]{2,1,0:T(8,128)(2,1)}), bf16[8,128,512]{2,1,0:T(8,128)(2,1)S(1)}, u32[]{:S(2)}, u32[]{:S(2)}) %all-to-all-start) | async-done | bytes 1048608 | tf_op jit(solution)/shard_map/all_to_all | solution.py:25
  36.8 1.0 fusion.2
  37.9 0.3 copy.35
  38.2 1.4 copy.36
  39.6 28.9 %all_to_all.22 = bf16[3,512,512]{2,0,1:T(4,128)(2,1)} all-to-all(bf16[3,512,512]{2,0,1:T(4,128)(2,1)S(1)} %copy.36), channel_id=1, replica_groups=mesh['fsdp'=8,'grp'=4] {'grp'}, dimensions={1} | all-to-all | bytes 3145728 | tf_op jit(solution)/shard_map/all_to_all | solution.py:51
  68.5 0.0 copy-done
  68.5 4.2 %convolution_convert_fusion = bf16[3,512,512]{2,1,0:T(8,128)(2,1)S(1)} fusion(bf16[3,512,512]{2,1,0:T(8,128)(2,1)S(1)} %copy-done, bf16[3,512,512]{2,1,0:T(8,128)(2,1)} %param.5, bf16[3,512,512]{2,0,1:T(4,128)(2,1)} %all_to_all.22), kind=kOutput, calls=%fused_computation.1 | convolution fusion | flops 1612185600 | bytes 6291456 | tf_op jit(solution)/shard_map/kab,kbc->kac/dot_general | solution.py:55
  72.7 1.4 copy.39
  74.0 28.1 %all_to_all.23 = bf16[3,512,512]{2,0,1:T(4,128)(2,1)S(1)} all-to-all(bf16[3,512,512]{2,0,1:T(4,128)(2,1)S(1)} %copy.39), channel_id=1, replica_groups=mesh['fsdp'=8,'grp'=4] {'grp'}, dimensions={1} | all-to-all | bytes 3145728 | tf_op jit(solution)/shard_map/all_to_all | solution.py:58
  102.2 2.2 %bitcast_convert_fusion = bf16[8,128,512]{2,0,1:T(8,128)(2,1)S(1)} fusion(bf16[3,4,128,512]{3,0,2,1:T(4,128)(2,1)S(1)} %bitcast.23, pred[3,8]{1,0:T(4,128)(4,1)S(1)} %iota_compare_fusion.1, pred[4,8]{1,0:T(4,128)(4,1)S(1)} %fusion.22), kind=kOutput, calls=%fused_computation | convolution fusion | flops 13107296 | bytes 2621496 | tf_op jit(solution)/shard_map/oks,kord->srd/dot_general | solution.py:60
  104.4 0.3 copy.42
  104.7 28.8 %all_to_all.24 = bf16[8,128,512]{2,1,0:T(8,128)(2,1)S(1)} all-to-all(bf16[8,128,512]{2,1,0:T(8,128)(2,1)S(1)} %copy.42), channel_id=1, replica_groups=mesh['fsdp'=8,'grp'=4] {'fsdp'}, dimensions={0} | all-to-all | bytes 2097152 | tf_op jit(solution)/shard_map/all_to_all | solution.py:63
  133.6 0.8 convolution_convert_fusion.4
  134.4 0.8 copy.44
  (5 shorter events, 0.0 us)
Async XLA Ops:
  0.0 68.5 %copy-start = (bf16[3,512,512]{2,1,0:T(8,128)(2,1)S(1)}, bf16[3,512,512]{2,1,0:T(8,128)(2,1)}, u32[]{:S(2)}) copy-start(bf16[3,512,512]{2,1,0:T(8,128)(2,1)} %param.6) | copy-start | bytes 4718596
  3.8 33.0 %all-to-all-start = ((bf16[8,128,512]{2,1,0:T(8,128)(2,1)}), bf16[8,128,512]{2,1,0:T(8,128)(2,1)S(1)}, u32[]{:S(2)}, u32[]{:S(2)}) async-start(bf16[8,128,512]{2,1,0:T(8,128)(2,1)} %copy.33), calls=%async_computation | async-start | bytes 2097152 | tf_op jit(solution)/shard_map/all_to_all | solution.py:25
where the time goes:
time: 136 us; the launch traced here: 135 us
  blocking collectives  85.9 us (63%)
  waiting for transfers between devices  25.4 us (19%)
  matrix products  9.85 us (7%)
  starting transfers between devices  7.28 us (5%)
  local copies, waits for them, and re-layouts  6.34 us (5%)
    all_to_all x1, blocking collectives, per_device(): lax.all_to_all(packed, 'grp', split_axis=1, concat_axis=1, tiled=True)  28.9 us
    all_to_all x1, blocking collectives, per_device(): lax.all_to_all(unpacked.reshape(columns * piece_rows, block_width), 'fsdp...  28.8 us
    all_to_all x1, blocking collectives, per_device(): lax.all_to_all(result, 'grp', split_axis=1, concat_axis=1, tiled=True)  28.1 us
    all_to_all x1, waiting for transfers between devices, per_device(): lax.all_to_all(outgoing.reshape(columns * piece_rows, block_width), 'fsdp...  25.4 us
    all_to_all x1, starting transfers between devices, per_device(): lax.all_to_all(outgoing.reshape(columns * piece_rows, block_width), 'fsdp...  7.28 us
    dot_general x1, matrix products, per_device(): jnp.einsum('kab,kbc->kac', left_product, right_factor, preferred_element_...  4.21 us
  transfers between devices with their start and end apart: 1, of which 1 were waited for; matrix products, arithmetic and copies ran while one was open for 0% of the time, Pallas kernels for 0%

commit v1 on v0

--- a/solution.py
+++ b/solution.py
@@ -55,7 +55,9 @@
     result = jnp.einsum(
         "kab,kbc->kac", left_product, right_factor, preferred_element_type=jnp.float32
     ).astype(jnp.bfloat16)
-    returned = lax.all_to_all(result, "grp", split_axis=1, concat_axis=1, tiled=True)
+    returned = jnp.concatenate(
+        lax.all_to_all(jnp.stack(jnp.split(result, lax.axis_size("grp"), 1), 0), "grp", 0, 0), 1
+    )
     returned = returned.reshape(slot_count, groups, piece_rows, block_width)
     unpacked = jnp.einsum(
         "oks,kord->srd", routing, returned, preferred_element_type=jnp.float32

time: 136 us -> 129 us (0.949)
  blocking collectives: 85.9 us -> 80.2 us
    all_to_all x1, blocking collectives: 28.1 us -> 22.5 us  [per_device(): lax.all_to_all(jnp.stack(jnp.split(result, lax.axis_size('grp'), 1), 0),...]
where the time goes in v1:
time: 129 us; the launch traced here: 128 us
  blocking collectives  80.2 us (62%)
  waiting for transfers between devices  25.4 us (20%)
  matrix products  9.55 us (7%)
  starting transfers between devices  7.28 us (6%)
  local copies, waits for them, and re-layouts  5.16 us (4%)
    all_to_all x1, blocking collectives, per_device(): lax.all_to_all(packed, 'grp', split_axis=1, concat_axis=1, tiled=True)  28.9 us
    all_to_all x1, blocking collectives, per_device(): lax.all_to_all(unpacked.reshape(columns * piece_rows, block_width), 'fsdp...  28.8 us
    all_to_all x1, waiting for transfers between devices, per_device(): lax.all_to_all(outgoing.reshape(columns * piece_rows, block_width), 'fsdp...  25.4 us
    all_to_all x1, blocking collectives, per_device(): lax.all_to_all(jnp.stack(jnp.split(result, lax.axis_size('grp'), 1), 0),...  22.5 us
    all_to_all x1, starting transfers between devices, per_device(): lax.all_to_all(outgoing.reshape(columns * piece_rows, block_width), 'fsdp...  7.28 us
    dot_general x1, matrix products, per_device(): jnp.einsum('kab,kbc->kac', left_product, right_factor, preferred_element_...  4.21 us
  transfers between devices with their start and end apart: 1, of which 1 were waited for; matrix products, arithmetic and copies ran while one was open for 0% of the time, Pallas kernels for 0%

profile of v1, /device:TPU:0, one launch (start us, length us, event | category | flops | bytes accessed | tf_op | source)
XLA Modules:
  0.0 128.3 jit_solution(15645042587539966793)
XLA Ops:
  0.0 0.0 copy-start
  0.0 0.8 reshape.94
  0.9 1.6 %convolution_convert_fusion.3 = bf16[8,128,512]{2,0,1:T(8,128)(2,1)S(1)} fusion(bf16[3,128,512]{2,1,0:T(8,128)(2,1)} %param.4, s32[3]{0:T(128)S(1)} %dynamic-slice_bitcast_fusion), kind=kOutput, calls=%fused_computation.8 | convolution fusion | flops 3670040 | bytes 1441804 | tf_op jit(solution)/shard_map/cj,jrd->crd/dot_general | solution.py:22
  2.5 1.3 %copy.20 = bf16[8,128,512]{2,1,0:T(8,128)(2,1)} copy(bf16[8,128,512]{2,0,1:T(8,128)(2,1)S(1)} %convolution_convert_fusion.3) | data formatting | bytes 2097152 | tf_op jit(solution)/shard_map/convert_element_type | solution.py:24
  3.8 7.3 %all-to-all-start = ((bf16[8,128,512]{2,1,0:T(8,128)(2,1)}), bf16[8,128,512]{2,1,0:T(8,128)(2,1)S(1)}, u32[]{:S(2)}, u32[]{:S(2)}) async-start(bf16[8,128,512]{2,1,0:T(8,128)(2,1)} %copy.20), calls=%async_computation | async-start | bytes 2097152 | tf_op jit(solution)/shard_map/all_to_all | solution.py:25
  11.1 0.1 convert_reduce_fusion.1
  11.2 0.2 convert_reduce_fusion
  11.4 25.4 %all-to-all-done = bf16[8,128,512]{2,1,0:T(8,128)(2,1)S(1)} async-done(((bf16[8,128,512]{2,1,0:T(8,128)(2,1)}), bf16[8,128,512]{2,1,0:T(8,128)(2,1)S(1)}, u32[]{:S(2)}, u32[]{:S(2)}) %all-to-all-start) | async-done | bytes 1048608 | tf_op jit(solution)/shard_map/all_to_all | solution.py:25
  36.8 1.0 fusion.2
  37.9 0.3 copy.22
  38.2 1.4 %copy.23 = bf16[3,512,512]{2,0,1:T(4,128)(2,1)S(1)} copy(bf16[3,512,512]{2,1,0:T(8,128)(2,1)S(1)} %bitcast.29) | data formatting | bytes 3145728 | tf_op jit(solution)/shard_map/reshape | solution.py:50
  39.6 28.9 %all_to_all.22 = bf16[3,512,512]{2,0,1:T(4,128)(2,1)} all-to-all(bf16[3,512,512]{2,0,1:T(4,128)(2,1)S(1)} %copy.23), channel_id=1, replica_groups=mesh['fsdp'=8,'grp'=4] {'grp'}, dimensions={1} | all-to-all | bytes 3145728 | tf_op jit(solution)/shard_map/all_to_all | solution.py:51
  68.5 0.0 copy-done
  68.5 4.2 %convolution_convert_fusion = bf16[3,512,512]{2,1,0:T(8,128)(2,1)S(1)} fusion(bf16[3,512,512]{2,1,0:T(8,128)(2,1)S(1)} %copy-done, bf16[3,512,512]{2,1,0:T(8,128)(2,1)} %param.5, bf16[3,512,512]{2,0,1:T(4,128)(2,1)} %all_to_all.22), kind=kOutput, calls=%fused_computation.1 | convolution fusion | flops 1612185600 | bytes 6291456 | tf_op jit(solution)/shard_map/kab,kbc->kac/dot_general | solution.py:55
  72.7 0.2 slice_bitcast_fusion.3
  72.9 0.2 pad_maximum_fusion
  73.1 22.5 %all_to_all.23 = bf16[4,3,128,512]{3,2,1,0:T(8,128)(2,1)S(1)} all-to-all(bf16[4,3,128,512]{3,2,1,0:T(8,128)(2,1)S(1)} %pad_maximum_fusion), channel_id=1, replica_groups=mesh['fsdp'=8,'grp'=4] {'grp'}, dimensions={0} | all-to-all | bytes 3145728 | tf_op jit(solution)/shard_map/all_to_all | solution.py:59
  95.6 1.9 %bitcast_convert_fusion = bf16[8,128,512]{2,0,1:T(8,128)(2,1)S(1)} fusion(bf16[3,4,128,512]{3,2,0,1:T(8,128)(2,1)S(1)} %bitcast.31, pred[3,8]{1,0:T(4,128)(4,1)S(1)} %iota_compare_fusion.1, pred[4,8]{1,0:T(4,128)(4,1)S(1)} %fusion.22), kind=kOutput, calls=%fused_computation | convolution fusion | flops 13107296 | bytes 2621496 | tf_op jit(solution)/shard_map/oks,kord->srd/dot_general | solution.py:62
  97.5 0.3 copy.27
  97.8 28.8 %all_to_all.24 = bf16[8,128,512]{2,1,0:T(8,128)(2,1)S(1)} all-to-all(bf16[8,128,512]{2,1,0:T(8,128)(2,1)S(1)} %copy.27), channel_id=1, replica_groups=mesh['fsdp'=8,'grp'=4] {'fsdp'}, dimensions={0} | all-to-all | bytes 2097152 | tf_op jit(solution)/shard_map/all_to_all | solution.py:65
  126.7 0.8 convolution_convert_fusion.4
  127.5 0.8 copy.29
  (5 shorter events, 0.0 us)
Async XLA Ops:
  0.0 68.5 %copy-start = (bf16[3,512,512]{2,1,0:T(8,128)(2,1)S(1)}, bf16[3,512,512]{2,1,0:T(8,128)(2,1)}, u32[]{:S(2)}) copy-start(bf16[3,512,512]{2,1,0:T(8,128)(2,1)} %param.6) | copy-start | bytes 4718596
  3.8 33.0 %all-to-all-start = ((bf16[8,128,512]{2,1,0:T(8,128)(2,1)}), bf16[8,128,512]{2,1,0:T(8,128)(2,1)S(1)}, u32[]{:S(2)}, u32[]{:S(2)}) async-start(bf16[8,128,512]{2,1,0:T(8,128)(2,1)} %copy.20), calls=%async_computation | async-start | bytes 2097152 | tf_op jit(solution)/shard_map/all_to_all | solution.py:25
